TPU v7x, 512 devices: a whole 4x8x8 slice. The times are simulated.
512 devices in a mesh: gx: 64 (over x, y, core), ta: 8 (over z).
Axes of the slice: x: 4, y: 8, z: 8, core: 2. Of those that a mesh axis runs over, the one named last changes fastest.
Arguments:
- master_flat: float32 [8388608], P(('gx', 'ta')), may hold values from -6 to 6
Outputs:
- serving_weight: bfloat16 [1, 8192, 1024], P(None, None, 'ta')
- channel_scale: float32 [1, 1024], P(None, 'ta')
All inputs are finite; a program needn't handle non-finite values.
Results may differ from a plain program's by a relative error of at most 0.015.
Values may be sent and summed in bfloat16 or wider, within the bound.
No kernel may reach another device: no remote copies, remote signals or barrier semaphores. Data moves between devices by JAX's collectives and lax.ppermute only.
A program may use at most 64 MiB of HBM per device.

v0:
```python
import jax
import jax.numpy as jnp
from jax import lax
from jax.sharding import PartitionSpec as P

D = 8192
KVH = 8
HEAD = 128
LAYERS = 1


def relayout(shard):
    regrouped = lax.all_to_all(shard, "ta", split_axis=1, concat_axis=0, tiled=True)
    complete = lax.all_gather(regrouped, "gx", axis=0, tiled=True)
    return complete.reshape(LAYERS, D, -1)


def shards(master_flat):
    kv_width = KVH * HEAD
    row_count = master_flat.shape[0] // kv_width
    rounded = master_flat.reshape(row_count, kv_width).astype(jnp.bfloat16)
    complete = relayout(rounded)
    widened = complete.astype(jnp.float32)
    channel_scale = jnp.max(jnp.abs(widened), axis=1)
    serving_weight = (widened / channel_scale[:, None, :]).astype(jnp.bfloat16)
    return (serving_weight, channel_scale)


def solution(mesh):
    in_specs = (P(("gx", "ta")),)
    out_specs = (P(None, None, "ta"), P(None, "ta"))
    return jax.shard_map(shards, mesh=mesh, in_specs=in_specs, out_specs=out_specs, check_vma=False)
```

profile of v0, /device:TPU:1, one launch (start us, length us, event | category | flops | bytes accessed | tf_op | source)
XLA Modules:
  0.0 117.4 jit_solution(15112434270394180846)
XLA Ops:
  7.2 0.0 all-gather.2.cloned.1.call-start
  7.2 0.8 convert_bitcast_fusion
  8.1 17.6 %all_to_all.16 = bf16[16,8,128]{2,0,1:T(8,128)(2,1)} all-to-all(bf16[16,8,128]{2,0,1:T(8,128)(2,1)S(1)} %copy.4), channel_id=1, replica_groups=mesh['gx'=64,'ta'=8] {'ta'}, dimensions={1} | all-to-all | bytes 65536 | tf_op jit(solution)/shard_map/all_to_all | solution.py:13
  25.7 0.0 all-gather.2.cloned.1.call-update
  25.7 80.8 %all-gather.2.cloned.1.call-done = bf16[8192,128]{1,0:T(8,128)(2,1)} async-done(((bf16[128,128]{1,0:T(8,128)(2,1)}), bf16[8192,128]{1,0:T(8,128)(2,1)}) %all-gather.2.cloned.1.call-update) | async-done | bytes 2097168 | tf_op jit(solution)/shard_map/all_gather | solution.py:14
  106.6 0.0 copy-start
  106.6 2.0 %fusion = f32[128]{0:T(128)S(1)} fusion(bf16[8192,128]{1,0:T(8,128)(2,1)} %all-gather.2.cloned.1.call-done), kind=kLoop, calls=%fused_computation.2 | loop fusion | flops 3145600 | bytes 2097664 | tf_op jit(solution)/shard_map/reduce_max | solution.py:24
  108.6 0.2 copy-done
  108.8 0.0 copy-start.1
  108.8 1.7 %fusion.2 = bf16[1,8192,128]{2,1,0:T(8,128)(2,1)} fusion(bf16[8192,128]{1,0:T(8,128)(2,1)S(1)} %copy-done, f32[128]{0:T(128)S(1)} %fusion), kind=kLoop, calls=%fused_computation.4 | loop fusion | flops 3145728 | bytes 4194816 | tf_op jit(solution)/shard_map/convert_element_type | solution.py:25
  110.5 0.0 copy-done.1
  (1 shorter events, 0.0 us)
Async XLA Ops:
  7.2 99.4 %all-gather.2.cloned.1.call-start = ((), (), s32[]{:S(2)}) async-start(), calls=%async_computation.1 | async-start | bytes 2129920 | tf_op jit(solution)/shard_map/all_gather | solution.py:14
  106.6 2.2 %copy-start = (bf16[8192,128]{1,0:T(8,128)(2,1)S(1)}, bf16[8192,128]{1,0:T(8,128)(2,1)}, u32[]{:S(2)}) copy-start(bf16[8192,128]{1,0:T(8,128)(2,1)} %all-gather.2.cloned.1.call-done) | copy-start | bytes 6291460
  108.8 1.7 %copy-start.1 = (f32[128]{0:T(128)}, f32[128]{0:T(128)S(1)}, u32[]{:S(2)}) copy-start(f32[128]{0:T(128)S(1)} %fusion) | copy-start | bytes 1540
Sparse Core Ops, SparseCore 0:
  25.8 80.6 all-gather.1
where the time goes:
time: 118 us; the launch traced here: 117 us
  waiting for transfers between devices  80.9 us (69%)
  blocking collectives  17.6 us (15%)
  between operations  14 us (12%)
  other arithmetic  4.6 us (4%)
    all_gather x1, waiting for transfers between devices, relayout(): complete = lax.all_gather(regrouped, 'gx', axis=0, tiled=True)  80.8 us
    all_to_all x1, blocking collectives, relayout(): lax.all_to_all(shard, 'ta', split_axis=1, concat_axis=0, tiled=True)  17.6 us
  transfers between devices with their start and end apart: 1, of which 1 were waited for; matrix products, arithmetic and copies ran while one was open for 0% of the time, Pallas kernels for 0%

commit v1 on v0

--- a/solution.py
+++ b/solution.py
@@ -11,7 +11,8 @@
 
 def relayout(shard):
     regrouped = lax.all_to_all(shard, "ta", split_axis=1, concat_axis=0, tiled=True)
-    complete = lax.all_gather(regrouped, "gx", axis=0, tiled=True)
+    copies = jnp.concatenate([regrouped] * lax.axis_size("gx"), axis=0)
+    complete = lax.all_to_all(copies, "gx", 0, 0, tiled=True)
     return complete.reshape(LAYERS, D, -1)
 
 

time: 118 us -> 85.9 us (0.73)
  waiting for transfers between devices: 80.9 us -> 0 us
  blocking collectives: 17.6 us -> 80.8 us
  between operations: 14 us -> 0.95 us
  other arithmetic: 4.6 us -> 3.34 us
    all_gather x1 -> x0, waiting for transfers between devices: 80.8 us -> none  [relayout(): complete = lax.all_gather(regrouped, 'gx', axis=0, tiled=True)]
    all_to_all x0 -> x1, blocking collectives: none -> 63.2 us  [relayout(): complete = lax.all_to_all(copies, 'gx', 0, 0, tiled=True)]
    reduce_max x1, other arithmetic: 2.03 us -> 0.32 us  [shards(): channel_scale = jnp.max(jnp.abs(widened), axis=1)]
  transfers between devices with their start and end apart: 1 -> 0, of which waited for: 1 -> 0; matrix products, arithmetic and copies ran while one was open for 0% -> 0% of each run, Pallas kernels for 0% -> 0%
where the time goes in v1:
time: 85.9 us; the launch traced here: 85.7 us
  blocking collectives  80.8 us (94%)
  other arithmetic  3.34 us (4%)
  between operations  0.95 us (1%)
    all_to_all x1, blocking collectives, relayout(): complete = lax.all_to_all(copies, 'gx', 0, 0, tiled=True)  63.2 us
    all_to_all x1, blocking collectives, relayout(): lax.all_to_all(shard, 'ta', split_axis=1, concat_axis=0, tiled=True)  17.5 us

profile of v1, /device:TPU:1, one launch (start us, length us, event | category | flops | bytes accessed | tf_op | source)
XLA Modules:
  0.0 85.7 jit_solution(17836894372241991580)
XLA Ops:
  0.6 0.8 convert_bitcast_fusion
  1.5 17.5 %all_to_all.25 = bf16[16,8,128]{2,0,1:T(8,128)(2,1)S(1)} all-to-all(bf16[16,8,128]{2,0,1:T(8,128)(2,1)S(1)} %copy.4), channel_id=1, replica_groups=mesh['gx'=64,'ta'=8] {'ta'}, dimensions={1} | all-to-all | bytes 65536 | tf_op jit(solution)/shard_map/all_to_all | solution.py:13
  20.0 63.2 %all_to_all.26 = bf16[64,128,128]{2,1,0:T(8,128)(2,1)S(1)} all-to-all(bf16[64,128,128]{2,1,0:T(8,128)(2,1)S(1)} %bitcast.77), channel_id=1, replica_groups=mesh['gx'=64,'ta'=8] {'gx'}, dimensions={0} | all-to-all | bytes 4194304 | tf_op jit(solution)/shard_map/all_to_all | solution.py:15
  83.2 0.3 abs_reduce_fusion
  83.5 0.0 copy-start
  83.5 0.5 convert_element_type.42
  84.0 0.0 copy-done
  84.1 1.7 %fusion = bf16[1,8192,128]{2,1,0:T(8,128)(2,1)} fusion(f32[128]{0:T(128)S(1)} %abs_reduce_fusion, f32[1,8192,128]{2,1,0:T(8,128)S(1)} %bitcast.76), kind=kLoop, calls=%fused_computation.1 | loop fusion | flops 2097152 | bytes 6291968 | tf_op jit(solution)/shard_map/convert_element_type | solution.py:26
  (65 shorter events, 0.7 us)
Async XLA Ops:
  83.5 0.5 copy-start
